TPU v7x, 32 devices: a whole 2x2x4 slice. The times are simulated.
32 devices in a mesh: rep: 2 (over x), dp: 16 (over y, z, core).
Axes of the slice: x: 2, y: 2, z: 4, core: 2. Of those that a mesh axis runs over, the one named last changes fastest.
Arguments:
- x: bfloat16 [32, 2048, 640], P(('rep', 'dp')), parts along dimension 0
- dy: bfloat16 [32, 2048, 640], P(('rep', 'dp')), parts along dimension 0
- w_gate: bfloat16 [2, 640, 2048], replicated
- w_up: bfloat16 [2, 640, 2048], replicated
- w_down: bfloat16 [2, 2048, 640], replicated
- m_w_gate: float32 [2, 640, 2048], replicated
- m_w_up: float32 [2, 640, 2048], replicated
- m_w_down: float32 [2, 2048, 640], replicated
- v_w_gate: float32 [2, 640, 2048], replicated
- v_w_up: float32 [2, 640, 2048], replicated
- v_w_down: float32 [2, 2048, 640], replicated
Outputs:
- output 1: bfloat16 [4, 640, 2048], P('rep'), parts along dimension 0
- output 2: bfloat16 [4, 640, 2048], P('rep'), parts along dimension 0
- output 3: bfloat16 [4, 2048, 640], P('rep'), parts along dimension 0
- output 4: float32 [4, 640, 2048], P('rep'), parts along dimension 0
- output 5: float32 [4, 640, 2048], P('rep'), parts along dimension 0
- output 6: float32 [4, 2048, 640], P('rep'), parts along dimension 0
- output 7: float32 [4, 640, 2048], P('rep'), parts along dimension 0
- output 8: float32 [4, 640, 2048], P('rep'), parts along dimension 0
- output 9: float32 [4, 2048, 640], P('rep'), parts along dimension 0
There are 2 independent parts. A program takes and returns all parts, laid end to end along the dimension named above; an argument that names none is the same for every part.
All inputs are finite; a program needn't handle non-finite values.
Results may differ from a plain program's by a relative error of at most 0.022.
Values are sent between devices in bfloat16 or wider.
A program may use at most 2.25 GiB of HBM per device.

v0:
```python
import jax
import jax.numpy as jnp
from jax import lax
from jax.sharding import PartitionSpec as P

NAMES = ("w_gate", "w_up", "w_down")


def matmul(a, w):
    return jnp.dot(a, w, preferred_element_type=jnp.float32).astype(jnp.bfloat16)


def normed(h):
    wide = h.astype(jnp.float32)
    scale = lax.rsqrt(jnp.mean(wide**2, -1, keepdims=True) + 1e-6)
    return (wide * scale).astype(jnp.bfloat16)


def layer(h, w):
    a = normed(h)
    gate = jnp.dot(a, w["w_gate"], preferred_element_type=jnp.float32)
    up = jnp.dot(a, w["w_up"], preferred_element_type=jnp.float32)
    return h + matmul((jax.nn.silu(gate) * up).astype(jnp.bfloat16), w["w_down"])


def adamw(w, m, v, g):
    m = 0.9 * m + 0.1 * g
    v = 0.95 * v + 0.05 * g * g
    step = m * lax.rsqrt(v + 1e-8) + 0.1 * w
    return (w - 0.02 * step).astype(jnp.bfloat16), m, v


def solution(mesh):
    def step(x, dy, *arrays):
        weights, m, v = (arrays[i : i + 3] for i in (0, 3, 6))
        layers = weights[0].shape[0]
        h, kept = x[0], []
        for number in range(layers):
            kept.append(h)
            h = layer(h, {name: w[number] for name, w in zip(NAMES, weights, strict=True)})
        by_h, summed = dy[0], [None] * layers
        for number in reversed(range(layers)):
            _, back = jax.vjp(lambda w, h: layer(h, w), {name: w[number] for name, w in zip(NAMES, weights, strict=True)}, kept[number])
            by_w, by_h = back(by_h)
            summed[number] = [lax.psum(by_w[name], "dp") for name in NAMES]
        gradients = [jnp.stack([summed[number][i] for number in range(layers)]).astype(jnp.float32) for i in range(3)]
        new = [adamw(w.astype(jnp.float32), m, v, g) for w, m, v, g in zip(weights, m, v, gradients, strict=True)]
        return tuple(one[which] for which in range(3) for one in new)

    return jax.shard_map(
        step,
        mesh=mesh,
        in_specs=(P(("rep", "dp"), None, None),) * 2 + (P(None, None, None),) * 9,
        out_specs=(P("rep", None, None),) * 9,
        check_vma=False,
    )
```

profile of v0, /device:TPU:0, one launch (start us, length us, event | category | flops | bytes accessed | tf_op | source)
XLA Modules:
  0.0 566.1 jit_solution(9864037031632442282)
XLA Ops:
  7.2 0.0 all-reduce.3.cloned.1.call-start
  7.2 3.0 copy.20
  10.2 0.6 fusion.30
  10.8 4.7 copy.21
  15.5 11.3 %convolution_convert_fusion.1 = bf16[2048,2048]{1,0:T(8,128)(2,1)} fusion(bf16[1,2048,640]{2,1,0:T(8,128)(2,1)} %param.12, bf16[2,2048,640]{2,1,0:T(8,128)(2,1)} %param.15), kind=kOutput, calls=%fused_computation.56 | convolution fusion | flops 5372903424 | bytes 13631488 | tf_op jit(solution)/shard_map/transpose(jvp())/dot_general | solution.py:10
  26.8 11.6 %fusion.68 = f32[2048,2048]{1,0:T(8,128)} fusion(bf16[2,640,2048]{2,1,0:T(8,128)(2,1)} %param.13, bf16[1,2048,640]{2,1,0:T(8,128)(2,1)S(1)} %copy-done.5, f32[2048]{0:T(1024)S(1)} %add_rsqrt_fusion), kind=kOutput, calls=%fused_computation.101 | convolution fusion | flops 5372641280 | bytes 22028288 | tf_op jit(solution)/shard_map/dot_general | solution.py:21
  38.4 16.9 %multiply_convert_fusion.1 = (bf16[2048,2048]{1,0:T(8,128)(2,1)}, f32[2048,2048]{1,0:T(8,128)}) fusion(f32[2048,2048]{1,0:T(8,128)} %fusion.68, bf16[2,640,2048]{2,1,0:T(8,128)(2,1)} %param.14, bf16[1,2048,640]{2,1,0:T(8,128)(2,1)} %param.11, f32[2048]{0:T(1024)S(1)} %add_rsqrt_fusion), kind=kOutput, calls=%fused_computation.17 | convolution fusion | flops 5397807104 | bytes 47194112 | tf_op jit(solution)/shard_map/dot_general | solution.py:22
  55.3 9.2 %fusion.34 = (f32[2048]{0:T(1024)S(1)}, bf16[2048,640]{0,1:T(8,128)(2,1)S(1)}) fusion(bf16[2048,2048]{1,0:T(8,128)(2,1)} %get-tuple-element.24, bf16[2,2048,640]{2,1,0:T(8,128)(2,1)} %param.15, bf16[1,2048,640]{1,2,0:T(8,128)(2,1)S(1)} %copy.20), kind=kOutput, calls=%fused_computation.64 | convolution fusion | flops 5375260672 | bytes 16261120 | tf_op jit(solution)/shard_map/dot_general | solution.py:10
  64.5 1.5 copy-done.3
  65.9 12.2 %fusion.57 = f32[2048,2048]{1,0:T(8,128)} fusion(bf16[2,640,2048]{2,1,0:T(8,128)(2,1)} %param.14, bf16[2048,640]{0,1:T(8,128)(2,1)S(1)} %get-tuple-element.27, f32[2048]{0:T(1024)S(1)} %fusion.92), kind=kOutput, calls=%fused_computation.90 | convolution fusion | flops 5372641280 | bytes 22028288 | tf_op jit(solution)/shard_map/jvp()/dot_general | solution.py:22
  78.1 25.1 %fusion.2 = (bf16[2048,2048]{1,0:T(8,128)(2,1)}, f32[2048,2048]{1,0:T(8,128)}) fusion(f32[2048,2048]{1,0:T(8,128)} %fusion.57, bf16[2048,2048]{1,0:T(8,128)(2,1)} %convolution_convert_fusion.1, bf16[2,640,2048]{2,1,0:T(8,128)(2,1)} %param.13, bf16[2048,640]{0,1:T(8,128)(2,1)} %copy-done.3, f32[2048]{0:T(1024)S(1)} %fusion.92), kind=kOutput, calls=%fused_computation.8 | convolution fusion | flops 5422972928 | bytes 55582720 | tf_op jit(solution)/shard_map/jvp()/dot_general | solution.py:21
  103.2 16.9 %fusion.49 = bf16[1,2048,640]{2,1,0:T(8,128)(2,1)} fusion(f32[2048,2048]{1,0:T(8,128)} %fusion.57, bf16[1,2048,640]{2,1,0:T(8,128)(2,1)} %param.12, f32[2048,2048]{1,0:T(8,128)} %get-tuple-element.29), kind=kOutput, calls=%fused_computation.82 | convolution fusion | flops 5395185664 | bytes 38797312 | tf_op jit(solution)/shard_map/transpose(jvp())/dot_general | solution.py:10
  120.2 13.3 %fusion.52 = bf16[1,640,2048]{2,1,0:T(8,128)(2,1)} fusion(bf16[2048,2048]{1,0:T(8,128)(2,1)} %convolution_convert_fusion.1, bf16[2048,640]{0,1:T(8,128)(2,1)} %copy-done.3, f32[2048]{0:T(1024)S(1)} %fusion.92, f32[2048,2048]{1,0:T(8,128)} %get-tuple-element.29), kind=kOutput, calls=%fused_computation.85 | convolution fusion | flops 5399117824 | bytes 30416896 | tf_op jit(solution)/shard_map/transpose(jvp())/dot_general | solution.py:22
  133.5 12.4 %fusion.38 = bf16[2048,640]{0,1:T(8,128)(2,1)} fusion(bf16[2048,2048]{1,0:T(8,128)(2,1)} %convolution_convert_fusion.1, bf16[2,640,2048]{2,1,0:T(8,128)(2,1)S(1)} %bitcast.77, f32[2048,2048]{1,0:T(8,128)} %get-tuple-element.29), kind=kOutput, calls=%fused_computation.72 | convolution fusion | flops 5395185664 | bytes 30408704 | tf_op jit(solution)/shard_map/transpose(jvp())/dot_general | solution.py:22
  145.9 10.9 %fusion.50 = bf16[1,640,2048]{2,1,0:T(8,128)(2,1)} fusion(bf16[2048,2048]{1,0:T(8,128)(2,1)} %get-tuple-element.28, bf16[2048,640]{0,1:T(8,128)(2,1)} %copy-done.3, f32[2048]{0:T(1024)S(1)} %fusion.92), kind=kOutput, calls=%fused_computation.83 | convolution fusion | flops 5372641280 | bytes 13639680 | tf_op jit(solution)/shard_map/transpose(jvp())/dot_general | solution.py:21
  156.9 8.5 %fusion.36 = (f32[2048]{0:T(1024)S(1)}, bf16[2048,640]{0,1:T(8,128)(2,1)S(1)}) fusion(bf16[2048,640]{0,1:T(8,128)(2,1)S(1)} %copy-done.4, bf16[2048,640]{0,1:T(8,128)(2,1)S(1)} %copy-done.12, bf16[2048,2048]{1,0:T(8,128)(2,1)} %get-tuple-element.28, bf16[2,640,2048]{2,1,0:T(8,128)(2,1)S(1)} %bitcast.75), kind=kOutput, calls=%fused_computation.66 | convolution fusion | flops 5375260672 | bytes 18882560 | tf_op jit(solution)/shard_map/transpose(jvp())/dot_general | solution.py:21
  165.4 2.0 fusion.54
  167.5 10.5 %fusion.51 = bf16[1,2048,640]{2,1,0:T(8,128)(2,1)} fusion(bf16[2048,2048]{1,0:T(8,128)(2,1)} %get-tuple-element.24, bf16[2048,640]{0,1:T(8,128)(2,1)S(1)} %fusion.54), kind=kOutput, calls=%fused_computation.84 | convolution fusion | flops 5370019840 | bytes 13631488 | tf_op jit(solution)/shard_map/transpose(jvp())/dot_general | solution.py:10
  178.0 7.3 %convolution_convert_fusion = bf16[2048,2048]{1,0:T(8,128)(2,1)S(1)} fusion(bf16[2048,640]{0,1:T(8,128)(2,1)S(1)} %fusion.54, bf16[2,2048,640]{2,1,0:T(8,128)(2,1)S(1)} %bitcast.79), kind=kOutput, calls=%fused_computation.55 | convolution fusion | flops 5372903424 | bytes 13631488 | tf_op jit(solution)/shard_map/transpose(jvp())/dot_general | solution.py:10
  185.3 13.9 %fusion.45 = bf16[1,640,2048]{2,1,0:T(8,128)(2,1)} fusion(bf16[2048,2048]{1,0:T(8,128)(2,1)S(1)} %convolution_convert_fusion, f32[2048,2048]{1,0:T(8,128)} %fusion.68, bf16[1,2048,640]{1,2,0:T(8,128)(2,1)S(1)} %copy-done.2, f32[2048]{0:T(1024)S(1)} %copy-done.10), kind=kOutput, calls=%fused_computation.80 | convolution fusion | flops 5399117824 | bytes 30416896 | tf_op jit(solution)/shard_map/transpose(jvp())/dot_general | solution.py:22
  199.2 19.0 %fusion.46 = bf16[1,640,2048]{2,1,0:T(8,128)(2,1)} fusion(f32[2048,2048]{1,0:T(8,128)} %fusion.68, f32[2048,2048]{1,0:T(8,128)} %get-tuple-element.25, bf16[2048,2048]{1,0:T(8,128)(2,1)} %copy-done.11, bf16[1,2048,640]{1,2,0:T(8,128)(2,1)S(1)} %copy-done.2, f32[2048]{0:T(1024)S(1)} %copy-done.10), kind=kOutput, calls=%fused_computation.81 | convolution fusion | flops 5420089344 | bytes 47194112 | tf_op jit(solution)/shard_map/transpose(jvp())/dot_general | solution.py:21
  218.2 283.4 %all-reduce.3.cloned.1.call-done = (bf16[1,640,2048]{2,1,0:T(8,128)(2,1)}, bf16[1,640,2048]{2,1,0:T(8,128)(2,1)}, bf16[1,640,2048]{2,1,0:T(8,128)(2,1)}, bf16[1,...) async-done(((bf16[1,640,2048]{2,1,0:T(8,128)(2,1)}, bf16[1,640,2048]{2,1,0:T(8,128)(2,1)}, bf16[1,640,2048]{2,1,0:T(8,128)(2,1)}, ...) | async-done | bytes 15728656 | tf_op jit(solution)/shard_map/psum | solution.py:45
  501.6 22.1 %fusion.23 = (bf16[2,2048,640]{2,1,0:T(8,128)(2,1)}, f32[2,2048,640]{2,1,0:T(8,128)}, f32[2,2048,640]{2,1,0:T(8,128)}) fusion(bf16[2,2048,640]{2,1,0:T(8,128)(2,1)} %param.15, bf16[1,2048,640]{2,1,0:T(8,128)(2,1)} %get-tuple-element.13, bf16[1,2048,640]{2,1,0:T(8,128)(2,1)} %get-tuple-element.14, f32[2,2048,640]{2,1,0:T(8,128)} %param.21, ...), kind=kLoop, calls=%fused_computation.44 | loop fusion | flops 49807360 | bytes 57671680 | tf_op jit(solution)/shard_map/convert_element_type | solution.py:30
  523.7 35.1 %fusion.15 = (bf16[2,640,2048]{2,1,0:T(8,128)(2,1)}, f32[2,640,2048]{2,1,0:T(8,128)}, f32[2,640,2048]{2,1,0:T(8,128)}, bf16[2,640,2048]{2,1,0:T(8,128)(2,1)}, f3...) fusion(bf16[2,640,2048]{2,1,0:T(8,128)(2,1)} %param.13, bf16[1,640,2048]{2,1,0:T(8,128)(2,1)S(1)} %copy-done.6, ...), kind=kLoop, calls=%fused_computation.36 | loop fusion | flops 99614720 | bytes 115343360 | tf_op jit(solution)/shard_map/convert_element_type | solution.py:30
  (44 shorter events, 0.1 us)
Async XLA Ops:
  7.2 494.5 %all-reduce.3.cloned.1.call-start = ((), (), s32[]{:S(2)}) async-start(), calls=%async_computation | async-start | bytes 31457280 | tf_op jit(solution)/shard_map/psum | solution.py:45
  10.2 45.0 %copy-start.1 = (bf16[1,2048,640]{1,2,0:T(8,128)(2,1)}, bf16[1,2048,640]{1,2,0:T(8,128)(2,1)S(1)}, u32[]{:S(2)}) copy-start(bf16[1,2048,640]{1,2,0:T(8,128)(2,1)S(1)} %copy.20) | copy-start | bytes 7864324
  10.8 27.6 %copy-start.9 = (f32[2048]{0:T(1024)}, f32[2048]{0:T(1024)S(1)}, u32[]{:S(2)}) copy-start(f32[2048]{0:T(1024)S(1)} %add_rsqrt_fusion) | copy-start | bytes 24580
  15.5 11.3 %copy-start.5 = (bf16[1,2048,640]{2,1,0:T(8,128)(2,1)S(1)}, bf16[1,2048,640]{2,1,0:T(8,128)(2,1)}, u32[]{:S(2)}) copy-start(bf16[1,2048,640]{2,1,0:T(8,128)(2,1)} %param.11) | copy-start | bytes 7864324
  64.4 1.5 copy-start.3
  64.4 1.5 copy-start.7
  78.1 55.4 %slice-start.2 = ((s8[5242880]{0:T(1024)(128)(4,1)}), s8[1048576]{0:T(1024)(128)(4,1)S(1)}, s32[]{:S(2)}) async-start(s8[5242880]{0:T(1024)(128)(4,1)} %bitcast.76), calls=%async_computation.3 | async-start | bytes 2097152
  103.2 30.2 %slice-start.3 = ((s8[5242880]{0:T(1024)(128)(4,1)}), s8[4194304]{0:T(1024)(128)(4,1)S(1)}, s32[]{:S(2)}) async-start(s8[5242880]{0:T(1024)(128)(4,1)} %bitcast.76), calls=%async_computation.4 | async-start | bytes 8388608
  120.2 36.7 %slice-start = ((s8[5242880]{0:T(1024)(128)(4,1)}), s8[4194304]{0:T(1024)(128)(4,1)S(1)}, s32[]{:S(2)}) async-start(s8[5242880]{0:T(1024)(128)(4,1)} %bitcast.74), calls=%async_computation.1 | async-start | bytes 8388608
  133.5 23.3 %slice-start.1 = ((s8[5242880]{0:T(1024)(128)(4,1)}), s8[1048576]{0:T(1024)(128)(4,1)S(1)}, s32[]{:S(2)}) async-start(s8[5242880]{0:T(1024)(128)(4,1)} %bitcast.74), calls=%async_computation.2 | async-start | bytes 2097152
  145.9 10.9 %copy-start.4 = (bf16[2048,640]{0,1:T(8,128)(2,1)S(1)}, bf16[2048,640]{0,1:T(8,128)(2,1)}, u32[]{:S(2)}) copy-start(bf16[2048,640]{0,1:T(8,128)(2,1)} %copy-done.3) | copy-start | bytes 7864324
  145.9 10.9 %copy-start.12 = (bf16[2048,640]{0,1:T(8,128)(2,1)S(1)}, bf16[2048,640]{0,1:T(8,128)(2,1)}, u32[]{:S(2)}) copy-start(bf16[2048,640]{0,1:T(8,128)(2,1)} %fusion.38) | copy-start | bytes 7864324
  156.9 8.5 %copy-start.8 = (f32[2048]{0:T(1024)S(1)}, f32[2048]{0:T(1024)}, u32[]{:S(2)}) copy-start(f32[2048]{0:T(1024)} %copy-done.7) | copy-start | bytes 24580
  156.9 8.5 %copy-start = (bf16[1,2048,640]{1,2,0:T(8,128)(2,1)S(1)}, bf16[1,2048,640]{1,2,0:T(8,128)(2,1)}, u32[]{:S(2)}) copy-start(bf16[1,2048,640]{1,2,0:T(8,128)(2,1)} %copy.21) | copy-start | bytes 7864324
  165.4 12.5 %slice-start.4 = ((s8[5242880]{0:T(1024)(128)(4,1)}), s8[1048576]{0:T(1024)(128)(4,1)S(1)}, s32[]{:S(2)}) async-start(s8[5242880]{0:T(1024)(128)(4,1)} %bitcast.78), calls=%async_computation.5 | async-start | bytes 2097152
  167.5 10.5 %slice-start.5 = ((s8[5242880]{0:T(1024)(128)(4,1)}), s8[4194304]{0:T(1024)(128)(4,1)S(1)}, s32[]{:S(2)}) async-start(s8[5242880]{0:T(1024)(128)(4,1)} %bitcast.78), calls=%async_computation.6 | async-start | bytes 8388608
  177.9 7.3 %copy-start.2 = (bf16[1,2048,640]{1,2,0:T(8,128)(2,1)S(1)}, bf16[1,2048,640]{1,2,0:T(8,128)(2,1)}, u32[]{:S(2)}) copy-start(bf16[1,2048,640]{1,2,0:T(8,128)(2,1)} %copy-done.1) | copy-start | bytes 7864324
  178.0 7.3 %copy-start.10 = (f32[2048]{0:T(1024)S(1)}, f32[2048]{0:T(1024)}, u32[]{:S(2)}) copy-start(f32[2048]{0:T(1024)} %copy-done.9) | copy-start | bytes 24580
  185.3 13.9 %copy-start.11 = (bf16[2048,2048]{1,0:T(8,128)(2,1)}, bf16[2048,2048]{1,0:T(8,128)(2,1)S(1)}, u32[]{:S(2)}) copy-start(bf16[2048,2048]{1,0:T(8,128)(2,1)S(1)} %convolution_convert_fusion) | copy-start | bytes 25165828
  501.6 22.1 %copy-start.6 = (bf16[1,640,2048]{2,1,0:T(8,128)(2,1)S(1)}, bf16[1,640,2048]{2,1,0:T(8,128)(2,1)}, u32[]{:S(2)}) copy-start(bf16[1,640,2048]{2,1,0:T(8,128)(2,1)} %get-tuple-element.9) | copy-start | bytes 7864324
Sparse Core Ops, SparseCore 0:
  218.4 283.2 all-reduce.2
where the time goes:
time: 575 us; the launch traced here: 566 us
  waiting for transfers between devices  283 us (49%)
  matrix products  199 us (35%)
  other arithmetic  59.8 us (10%)
  between operations  14.7 us (3%)
  local copies, waits for them, and re-layouts  9.26 us (2%)
    psum x1, waiting for transfers between devices, step(): summed[number] = [lax.psum(by_w[name], 'dp') for name in NAMES]  283 us
    dot_general x5, matrix products, layer(): gate = jnp.dot(a, w['w_gate'], preferred_element_type=jnp.float32)  75.1 us
    dot_general x5, matrix products, layer(): up = jnp.dot(a, w['w_up'], preferred_element_type=jnp.float32)  68.7 us
    convert_element_type x2, other arithmetic, adamw(): return ((w - 0.02 * step).astype(jnp.bfloat16), m, v)  57.1 us
    dot_general x5, matrix products, matmul(): jnp.dot(a, w, preferred_element_type=jnp.float32).astype(jnp.bfloat16)  55.1 us
  transfers between devices with their start and end apart: 1, of which 1 were waited for; matrix products, arithmetic and copies ran while one was open for 0% of the time, Pallas kernels for 0%

commit v1 on v0

v1 whole, which is shorter than its diff:
```python
import jax
import jax.numpy as jnp
from jax import lax
from jax.experimental import pallas as pl
from jax.experimental.pallas import tpu as pltpu
from jax.sharding import PartitionSpec as P

NAMES = ("w_gate", "w_up", "w_down")
F32, BF16 = jnp.float32, jnp.bfloat16
T, D, FF, L = 2048, 640, 2048, 2
C = 256
PER = FF // C
N = L * PER
NS = 6
R = 3 * D
Q = R // 4
STEPS = N + 5
MESH = pl.DeviceIdType.MESH
NT = (((1,), (1,)), ((), ()))


def normed(h):
    wide = h.astype(F32)
    scale = lax.rsqrt(jnp.mean(wide**2, -1, keepdims=True) + 1e-6)
    return (wide * scale).astype(BF16)


def dot(a, b):
    return jnp.dot(a, b, preferred_element_type=F32)


def add(*terms):
    total = terms[0].astype(F32)
    for term in terms[1:]:
        total = total + term.astype(F32)
    return total.astype(BF16)


def backward_kernel(
    a1, a1t, dy, dyt, h1, a0, a0t, wg, wu, wd, out_g, out_u, out_d,
    A, AT, DY, DYT, H, DA, ACT, DG, DU, WG, WU, WD, OT,
    G, DD, YR, ZR1, XR, ZR2, MR, YX, ST1, ST2, ST3,
    ld, ws, outs, sent, got,
):
    rep, dp = lax.axis_index("rep"), lax.axis_index("dp")
    core, z, y = lax.rem(dp, 2), lax.rem(dp // 2, 4), dp // 8
    at = lambda y, z, core: (rep, (y * 4 + z) * 2 + core)
    zo = z + 1 - 2 * lax.rem(z, 2)
    partner, across, end, mid = at(y, z, 1 - core), at(1 - y, z, core), at(y, zo, core), at(y, 3 - z, core)
    inner = (z == 1) | (z == 2)
    outer = (z == 0) | (z == 3)
    mi = lax.rem(z + 1, 2)
    mine_y, their_y = pl.multiple_of(y * Q, 16), pl.multiple_of((1 - y) * Q, 16)
    mine_m, their_m = pl.multiple_of(2 * Q + mi * Q, 16), pl.multiple_of(2 * Q + (1 - mi) * Q, 16)
    mine_y, their_y, mine_m, their_m = (pl.ds(start, Q) for start in (mine_y, their_y, mine_m, their_m))
    low = pl.ds(2 * Q, 2 * Q)

    def loads():
        return [pltpu.make_async_copy(s, d, ld.at[i]) for i, (s, d) in enumerate(((a1, A), (dy, DY), (a1t, AT), (dyt, DYT), (h1, H)))]

    def weights(i):
        layer, j, s = L - 1 - i // PER, lax.rem(i, PER), lax.rem(i, 2)
        cols = pl.ds(pl.multiple_of(j * C, C), C)
        return [
            pltpu.make_async_copy(wg.at[layer, :, cols], WG.at[s], ws.at[s, 0]),
            pltpu.make_async_copy(wu.at[layer, :, cols], WU.at[s], ws.at[s, 1]),
            pltpu.make_async_copy(wd.at[layer, cols, :], WD.at[s], ws.at[s, 2]),
        ]

    for copy in loads() + weights(0):
        copy.start()

    barrier = pltpu.get_barrier_semaphore()
    for device in (partner, across, end):
        pl.semaphore_signal(barrier, inc=1, device_id=device, device_id_type=MESH)

    @pl.when(inner)
    def _():
        pl.semaphore_signal(barrier, inc=1, device_id=mid, device_id_type=MESH)

    pl.semaphore_wait(barrier, 3 + inner.astype(jnp.int32))
    DA[...] = jnp.zeros_like(DA)
    for copy in loads():
        copy.wait()

    def copies(q):
        def remote(n, src, dst, device):
            return pltpu.make_async_remote_copy(
                src_ref=src, dst_ref=dst, send_sem=sent.at[n, q], recv_sem=got.at[n, q], device_id=device, device_id_type=MESH
            )

        own = G.at[q, core]
        made = dict(
            d1=lambda: remote(0, G.at[q, 1 - core], DD.at[q], partner),
            y1=lambda: remote(1, ST1.at[q], YR.at[q], across),
            z2=lambda: remote(2, ST2.at[q], ZR2.at[q], end),
            z1=lambda: remote(3, ST3.at[q], ZR1.at[q], end),
            m2=lambda: remote(4, ST2.at[q, pl.ds(0, Q)], MR.at[q], mid),
            x1=lambda: remote(5, ST3.at[q], XR.at[q], mid),
            y2=lambda: remote(6, ST2.at[q, pl.ds(Q, Q)], YX.at[q], across),
            f1=lambda: remote(7, own.at[mine_y], own.at[mine_y], end),
            f2=lambda: remote(8, own.at[mine_y], own.at[mine_y], across),
            g1=lambda: remote(9, own.at[mine_m], own.at[mine_m], mid),
            g2=lambda: remote(10, own.at[mine_m], own.at[mine_m], end),
            g3=lambda: remote(11, own.at[their_m], own.at[their_m], end),
            d2=lambda: remote(12, own, own, partner),
        )
        return lambda name: made[name]()

    def out_copies(c):
        layer, j, q, s = L - 1 - c // PER, lax.rem(c, PER), lax.rem(c, NS), lax.rem(c, 2)
        made = []
        for half in range(2):
            cols = pl.ds(pl.multiple_of(j * C + half * 128, 128), 128)
            made.append(pltpu.make_async_copy(G.at[q, half, pl.ds(0, D)], out_g.at[layer, :, cols], outs.at[s, half]))
            made.append(pltpu.make_async_copy(G.at[q, half, pl.ds(D, D)], out_u.at[layer, :, cols], outs.at[s, 2 + half]))
        rows = pl.ds(pl.multiple_of(j * C, C), C)
        made.append(pltpu.make_async_copy(OT.at[s], out_d.at[layer, rows, :], outs.at[s, 4]))
        return made

    def stage_d1(q, c):
        c("d1").start()

    def stage_first(q, c):
        c("d1").wait()
        ST1[q] = add(G[q, core, their_y], DD[q, their_y])
        c("y1").start()

        @pl.when(outer)
        def _():
            ST2[q] = add(G[q, core, low], DD[q, low])
            c("z2").start()

    def stage_z1(q, c):
        @pl.when(outer)
        def _():
            c("y1").wait_recv()
            ST3[q] = add(G[q, core, mine_y], DD[q, mine_y], YR[q])
            c("z1").start()

    def stage_m2(q, c):
        @pl.when(inner)
        def _():
            c("z2").wait_recv()
            ST2[q, pl.ds(0, Q)] = add(G[q, core, their_m], DD[q, their_m], ZR2[q, pl.ds(pl.multiple_of((1 - mi) * Q, 16), Q)])
            c("m2").start()

    def stage_x1(q, c):
        @pl.when(inner)
        def _():
            c("y1").wait_recv()
            c("z1").wait_recv()
            ST3[q] = add(G[q, core, mine_y], DD[q, mine_y], YR[q], ZR1[q])
            c("x1").start()

    def stage_y2(q, c):
        @pl.when(inner)
        def _():
            c("m2").wait_recv()
            ST2[q, pl.ds(Q, Q)] = add(G[q, core, mine_m], DD[q, mine_m], ZR2[q, pl.ds(pl.multiple_of(mi * Q, 16), Q)], MR[q])
            c("y2").start()

    def stage_f(q, c):
        @pl.when(inner)
        def _():
            c("x1").wait()
            G[q, core, mine_y] = add(ST3[q], XR[q])
            c("f1").start()
            c("f2").start()

    def stage_g(q, c):
        @pl.when(inner)
        def _():
            c("y2").wait()
            G[q, core, mine_m] = add(ST2[q, pl.ds(Q, Q)], YX[q])
            c("g1").start()
            c("g2").start()

    def stage_f2(q, c):
        @pl.when(outer)
        def _():
            c("f1").wait_recv()
            c("f2").start()

    def stage_g3(q, c):
        @pl.when(inner)
        def _():
            c("g1").wait_recv()
            c("g3").start()

    def stage_d2(q, c):
        c("f2").wait_recv()

        @pl.when(outer)
        def _():
            c("g2").wait_recv()
            c("g3").wait_recv()

        c("d2").start()

    def stage_end(q, c):
        c("d2").wait()
        for name in ("y1", "f2"):
            c(name).wait_send()

        @pl.when(outer)
        def _():
            for name in ("z2", "z1"):
                c(name).wait_send()

        @pl.when(inner)
        def _():
            for name in ("m2", "f1", "g1", "g2", "g3"):
                c(name).wait_send()

    STAGES = {
        0: stage_d1, 1: stage_first, 4: stage_z1, 5: stage_m2, 7: stage_x1, 8: stage_y2,
        10: stage_f, 11: stage_g, 13: stage_f2, 14: stage_g3, 17: stage_d2,
    }
    END = 18

    def tick(i, k):
        for when, stage in sorted(STAGES.items(), reverse=True):
            if when % 4 != k:
                continue
            c = i - 1 - when // 4

            @pl.when((c >= 0) & (c < N))
            def _(c=c, stage=stage):
                q = lax.rem(c, NS)
                stage(q, copies(q))

        if END % 4 == k:
            c = i - 1 - END // 4

            @pl.when((c >= 0) & (c < N))
            def _():
                q, s = lax.rem(c, NS), lax.rem(c, 2)

                @pl.when(c >= 1)
                def _():
                    for copy in out_copies(c - 1):
                        copy.wait()

                stage_end(q, copies(q))
                for half in range(2):
                    OT[s, pl.ds(half * 128, 128), :] = G[q, half, pl.ds(2 * D, D)].astype(F32).T.astype(BF16)
                for copy in out_copies(c):
                    copy.start()

    def tokens(s, first):
        def block(b, _):
            rows = pl.ds(pl.multiple_of(first + b * 512, 512), 512)
            a = A[rows]
            gate, up = dot(a, WG[s]), dot(a, WU[s])
            dact = lax.dot_general(DY[rows], WD[s], NT, preferred_element_type=F32).astype(BF16).astype(F32)
            sig = 1.0 / (1.0 + jnp.exp(-gate))
            silu = gate * sig
            ACT[rows] = (silu * up).astype(BF16)
            DU[rows] = (dact * silu).astype(BF16)
            DG[rows] = (dact * up * (sig + silu * (1.0 - sig))).astype(BF16)
            return _

        lax.fori_loop(0, 2, block, None)

    def gradient(q, which, left, right):
        def block(b, _):
            rows = pl.multiple_of(b * 128, 128)
            g = dot(left[pl.ds(rows, 128)], right[...]).astype(BF16)
            to = pl.ds(pl.multiple_of(which * D + rows, 128), 128)
            G[q, 0, to] = g[:, :128]
            G[q, 1, to] = g[:, 128:]
            return _

        lax.fori_loop(0, D // 128, block, None)

    def switch():
        copies = [pltpu.make_async_copy(a0, A, ld.at[0]), pltpu.make_async_copy(a0t, AT, ld.at[2])]
        for copy in copies:
            copy.start()

        def block(b, _):
            rows = pl.ds(pl.multiple_of(b * 256, 256), 256)
            h = H[rows].astype(F32)
            da = DA[rows].astype(BF16).astype(F32)
            scale = lax.rsqrt(jnp.mean(h * h, -1, keepdims=True) + 1e-6)
            along = jnp.sum(da * h, -1, keepdims=True) * (1.0 / D)
            dh = (scale * (da - h * (scale * scale * along))).astype(BF16)
            new = DY[rows].astype(F32) + dh.astype(F32)
            DY[rows] = new.astype(BF16)
            DYT[:, rows] = new.T.astype(BF16)
            return _

        lax.fori_loop(0, T // 256, block, None)
        for copy in copies:
            copy.wait()

    def step(i, _):
        busy = i < N
        s, q = lax.rem(i, 2), lax.rem(i, NS)

        tick(i, 0)

        @pl.when(i == PER)
        def _():
            switch()

        @pl.when(busy)
        def _():
            for copy in weights(i):
                copy.wait()

            @pl.when(i + 1 < N)
            def _():
                for copy in weights(i + 1):
                    copy.start()

            tokens(s, 0)

        tick(i, 1)

        @pl.when(busy)
        def _():
            tokens(s, 1024)

        tick(i, 2)

        @pl.when(busy)
        def _():
            gradient(q, 0, AT, DG)
            gradient(q, 1, AT, DU)

        tick(i, 3)

        @pl.when(busy)
        def _():
            gradient(q, 2, DYT, ACT)

        @pl.when(i < PER)
        def _():
            def block(b, _):
                rows = pl.ds(pl.multiple_of(b * 512, 512), 512)
                DA[rows] += lax.dot_general(DG[rows], WG[s], NT, preferred_element_type=F32) + lax.dot_general(
                    DU[rows], WU[s], NT, preferred_element_type=F32
                )
                return _

            lax.fori_loop(0, T // 512, block, None)

        return _

    lax.fori_loop(0, STEPS, step, None)
    for copy in out_copies(N - 1):
        copy.wait()


def backward(a1, a1t, dy, dyt, h1, a0, a0t, wg, wu, wd):
    vm = pltpu.VMEM
    return pl.pallas_call(
        backward_kernel,
        out_shape=[jax.ShapeDtypeStruct(w.shape, BF16) for w in (wg, wu, wd)],
        in_specs=[pl.BlockSpec(memory_space=pl.ANY)] * 10,
        out_specs=[pl.BlockSpec(memory_space=pl.ANY)] * 3,
        scratch_shapes=[
            vm((T, D), BF16), vm((D, T), BF16), vm((T, D), BF16), vm((D, T), BF16), vm((T, D), BF16), vm((T, D), F32),
            vm((T, C), BF16), vm((T, C), BF16), vm((T, C), BF16),
            vm((2, D, C), BF16), vm((2, D, C), BF16), vm((2, C, D), BF16), vm((2, C, D), BF16),
            vm((NS, 2, R, 128), BF16), vm((NS, R, 128), BF16), vm((NS, Q, 128), BF16), vm((NS, Q, 128), BF16), vm((NS, Q, 128), BF16),
            vm((NS, 2 * Q, 128), BF16), vm((NS, Q, 128), BF16), vm((NS, Q, 128), BF16),
            vm((NS, Q, 128), BF16), vm((NS, 2 * Q, 128), BF16), vm((NS, Q, 128), BF16),
            pltpu.SemaphoreType.DMA((5,)), pltpu.SemaphoreType.DMA((2, 3)), pltpu.SemaphoreType.DMA((2, 5)),
            pltpu.SemaphoreType.DMA((13, NS)), pltpu.SemaphoreType.DMA((13, NS)),
        ],
        compiler_params=pltpu.CompilerParams(collective_id=0, has_side_effects=True, vmem_limit_bytes=60 * 2**20),
    )(a1, a1t, dy, dyt, h1, a0, a0t, wg, wu, wd)


def adamw(w, m, v, g):
    m = 0.9 * m + 0.1 * g
    v = 0.95 * v + 0.05 * g * g
    step = m * lax.rsqrt(v + 1e-8) + 0.1 * w
    return (w - 0.02 * step).astype(BF16), m, v


def solution(mesh):
    def step(x, dy, *arrays):
        weights, m, v = (arrays[i : i + 3] for i in (0, 3, 6))
        wg, wu, wd = weights
        x, dy = x[0], dy[0]
        a0 = normed(x)
        act = (jax.nn.silu(dot(a0, wg[0])) * dot(a0, wu[0])).astype(BF16)
        h1 = x + dot(act, wd[0]).astype(BF16)
        a1 = normed(h1)
        gradients = backward(a1, a1.T, dy, dy.T, h1, a0, a0.T, wg, wu, wd)
        new = [adamw(w.astype(F32), m, v, g.astype(F32)) for w, m, v, g in zip(weights, m, v, gradients, strict=True)]
        return tuple(one[which] for which in range(3) for one in new)

    return jax.shard_map(
        step,
        mesh=mesh,
        in_specs=(P(("rep", "dp"), None, None),) * 2 + (P(None, None, None),) * 9,
        out_specs=(P("rep", None, None),) * 9,
        check_vma=False,
    )
```

time: 575 us -> 342 us (0.59); the launches traced: 566 us -> 341 us
  waiting for transfers between devices: 283 us -> 0 us
  Pallas kernels: 0 us -> 214 us
  matrix products: 199 us -> 31.9 us
  other arithmetic: 59.8 us -> 74.5 us
  between operations: 14.7 us -> 0.67 us
  local copies, waits for them, and re-layouts: 9.26 us -> 20.5 us
    psum x1 -> x0, waiting for transfers between devices: 283 us -> none  [step(): summed[number] = [lax.psum(by_w[name], 'dp') for name in NAMES]]
    pallas_call x0 -> x1, Pallas kernels: none -> 214 us  [backward(): pl.pallas_call(backward_kernel, out_shape=[jax.ShapeDtypeStruct(w.shape,...]
    dot_general x15 -> x2, matrix products: 199 us -> 31.9 us  [dot(): return jnp.dot(a, b, preferred_element_type=F32)]
    convert_element_type x2 -> x4, other arithmetic: 57.1 us -> 67.8 us  [the longest x2 61.7 us: adamw(): return ((w - 0.02 * step).astype(BF16), m, v)]
    convert_element_type x0 -> x2, local copies, waits for them, and re-layouts: none -> 8.75 us  [normed(): return (wide * scale).astype(BF16)]
    transpose x0 -> x2, other arithmetic: none -> 6.1 us  [step(): gradients = backward(a1, a1.T, dy, dy.T, h1, a0, a0.T, wg, wu, wd)]
  transfers between devices with their start and end apart: 1 -> 0, of which waited for: 1 -> 0; matrix products, arithmetic and copies ran while one was open for 0% -> 0% of each run, Pallas kernels for 0% -> 0%
where the time goes in v1:
time: 342 us; the launch traced here: 341 us
  Pallas kernels  214 us (63%)
  other arithmetic  74.5 us (22%)
  matrix products  31.9 us (9%)
  local copies, waits for them, and re-layouts  20.5 us (6%)
    pallas_call x1, Pallas kernels, backward(): pl.pallas_call(backward_kernel, out_shape=[jax.ShapeDtypeStruct(w.shape,...  214 us
    convert_element_type x2, other arithmetic, adamw(): return ((w - 0.02 * step).astype(BF16), m, v)  61.7 us
    dot_general x2, matrix products, dot(): return jnp.dot(a, b, preferred_element_type=F32)  31.9 us
    convert_element_type x2, local copies, waits for them, and re-layouts, normed(): return (wide * scale).astype(BF16)  8.75 us
    unnamed x2, local copies, waits for them, and re-layouts  7.37 us

profile of v1, /device:TPU:0, one launch (start us, length us, event | category | flops | bytes accessed | tf_op | source)
XLA Modules:
  0.0 341.1 jit_solution(16009975984089565775)
XLA Ops:
  0.6 3.0 copy.20
  3.6 0.6 fusion.15
  4.2 12.4 %fusion.24 = f32[2048,2048]{1,0:T(8,128)} fusion(bf16[2,640,2048]{2,1,0:T(8,128)(2,1)} %wg.1, bf16[1,2048,640]{2,1,0:T(8,128)(2,1)} %param.11, f32[2048]{0:T(1024)S(1)} %add_rsqrt_fusion.1), kind=kOutput, calls=%fused_computation.41 | convolution fusion | flops 5372641280 | bytes 22028288 | tf_op jit(solution)/shard_map/dot_general | solution.py:29
  16.6 19.6 %fusion.17 = (f32[2048]{0:T(1024)S(1)}, bf16[2048,640]{0,1:T(8,128)(2,1)}) fusion(bf16[2,2048,640]{2,1,0:T(8,128)(2,1)} %wd.1, f32[2048,2048]{1,0:T(8,128)} %fusion.24, bf16[2,640,2048]{2,1,0:T(8,128)(2,1)} %wu.1, bf16[1,2048,640]{2,1,0:T(8,128)(2,1)} %param.11, f32[2048]{0:T(1024)S(1)} %add_rsqrt_fusion.1, bf16[1,2048,640]{1,2,0:T(8,128)(2,1)S(1)} %copy.20), kind=kOutput, calls=%fused_computation.34 | convolution fusion | flops 10776999936 | bytes 29900800 | tf_op jit(solution)/shard_map/dot_general | solution.py:29
  36.1 4.0 %fusion.49.a1t = bf16[640,2048]{1,0:T(8,128)(2,1)} fusion(f32[2048]{0:T(1024)S(1)} %add_rsqrt_fusion, bf16[2048,640]{0,1:T(8,128)(2,1)} %get-tuple-element.25), kind=kLoop, calls=%fused_computation.51 | loop fusion | flops 3932160 | bytes 5251072 | tf_op jit(solution)/shard_map/transpose | solution.py:394
  40.1 4.0 %fusion.18 = bf16[2048,640]{0,1:T(8,128)(2,1)} fusion(bf16[2048,640]{0,1:T(8,128)(2,1)} %get-tuple-element.25, f32[2048]{0:T(1024)S(1)} %add_rsqrt_fusion), kind=kLoop, calls=%fused_computation.35 | loop fusion | flops 3932160 | bytes 5251072 | tf_op jit(solution)/shard_map/convert_element_type | solution.py:25
  44.1 4.4 %copy.22.a1 = bf16[2048,640]{1,0:T(8,128)(2,1)} copy(bf16[2048,640]{0,1:T(8,128)(2,1)} %fusion.18) | data formatting | bytes 5242880 | tf_op jit(solution)/shard_map/convert_element_type | solution.py:25
  48.4 4.4 %copy.24.h1 = bf16[2048,640]{1,0:T(8,128)(2,1)} copy(bf16[2048,640]{0,1:T(8,128)(2,1)} %get-tuple-element.25) | data formatting | bytes 5242880 | tf_op jit(solution)/shard_map/add | solution.py:392
  52.8 2.1 fusion.16
  54.9 4.4 %copy.25.a0 = bf16[2048,640]{1,0:T(8,128)(2,1)} copy(bf16[2048,640]{0,1:T(8,128)(2,1)} %fusion.16) | data formatting | bytes 5242880 | tf_op jit(solution)/shard_map/convert_element_type | solution.py:25
  59.3 2.1 fusion.48.a0t
  61.4 4.4 %copy.21 = bf16[1,2048,640]{1,2,0:T(8,128)(2,1)} copy(bf16[1,2048,640]{2,1,0:T(8,128)(2,1)} %param.12) | data formatting | bytes 5242880 | tf_op args[1]
  65.8 213.5 %shard_map.178 = (bf16[2,640,2048]{2,1,0:T(8,128)(2,1)}, bf16[2,640,2048]{2,1,0:T(8,128)(2,1)}, bf16[2,2048,640]{2,1,0:T(8,128)(2,1)}) custom-call(bf16[2048,640]{1,0:T(8,128)(2,1)} %copy.22.a1, bf16[640,2048]{1,0:T(8,128)(2,1)} %fusion.49.a1t, bf16[2048,640]{1,0:T(8,128)(2,1)} %bitcast.40, bf16[640,2048]{1,0:T(8,128)(2,1)} %bitcast.41, ...), custom_call_target="tpu_custom_call" | custom-call | tf_op jit(solution)/shard_map/pallas_call | solution.py:359
  279.3 39.9 %fusion.2 = (bf16[2,640,2048]{2,1,0:T(8,128)(2,1)}, f32[2,640,2048]{2,1,0:T(8,128)}, f32[2,640,2048]{2,1,0:T(8,128)}, bf16[2,640,2048]{2,1,0:T(8,128)(2,1)}, f32...) fusion(bf16[2,640,2048]{2,1,0:T(8,128)(2,1)} %wg.1, bf16[2,640,2048]{2,1,0:T(8,128)(2,1)} %get-tuple-element.12, ...), kind=kLoop, calls=%fused_computation.15 | loop fusion | flops 83886080 | bytes 115343360 | tf_op jit(solution)/shard_map/convert_element_type | solution.py:382
  319.3 21.8 %fusion.10 = (bf16[2,2048,640]{2,1,0:T(8,128)(2,1)}, f32[2,2048,640]{2,1,0:T(8,128)}, f32[2,2048,640]{2,1,0:T(8,128)}) fusion(bf16[2,2048,640]{2,1,0:T(8,128)(2,1)} %wd.1, bf16[2,2048,640]{2,1,0:T(8,128)(2,1)} %get-tuple-element.14, f32[2,2048,640]{2,1,0:T(8,128)} %param.21, f32[2,2048,640]{2,1,0:T(8,128)} %param.18), kind=kLoop, calls=%fused_computation.23 | loop fusion | flops 41943040 | bytes 57671680 | tf_op jit(solution)/shard_map/convert_element_type | solution.py:382
  (2 shorter events, 0.0 us)

commit v2 on v1

v2 whole, which is shorter than its diff:
```python
import jax
import jax.numpy as jnp
from jax import lax
from jax.experimental import pallas as pl
from jax.experimental.pallas import tpu as pltpu
from jax.sharding import PartitionSpec as P

NAMES = ("w_gate", "w_up", "w_down")
F32, BF16 = jnp.float32, jnp.bfloat16
T, D, FF, L = 2048, 640, 2048, 2
C = 256
PER = FF // C
N = L * PER
PIECES = 2 * N
NS = 10
R = 3 * D // 2
Q = R // 4
MESH = pl.DeviceIdType.MESH
NT = (((1,), (1,)), ((), ()))


def normed(h):
    wide = h.astype(F32)
    scale = lax.rsqrt(jnp.mean(wide**2, -1, keepdims=True) + 1e-6)
    return (wide * scale).astype(BF16)


def dot(a, b):
    return jnp.dot(a, b, preferred_element_type=F32)


def dot_nt(a, b):
    return lax.dot_general(a, b, NT, preferred_element_type=F32)


def sigmoid(a):
    return 0.5 * jnp.tanh(0.5 * a) + 0.5


def add(*terms):
    total = terms[0].astype(F32)
    for term in terms[1:]:
        total = total + term.astype(F32)
    return total.astype(BF16)


def step_kernel(
    x, dy, wg, wu, wd, out_g, out_u, out_d,
    A, AT, DY, DYT, H, DA, ACT, DGU, ACTF, WF, WU, WFD, WGU, WD, OT,
    G, DD, YR, ZR1, XR, ZR2, MR, YX, ST1, ST2, ST3,
    ld, ws, outs, sent, got,
):
    rep, dp = lax.axis_index("rep"), lax.axis_index("dp")
    core, z, y = lax.rem(dp, 2), lax.rem(dp // 2, 4), dp // 8
    at = lambda y, z, core: (rep, (y * 4 + z) * 2 + core)
    zo = z + 1 - 2 * lax.rem(z, 2)
    partner, across, end, mid = at(y, z, 1 - core), at(1 - y, z, core), at(y, zo, core), at(y, 3 - z, core)
    inner = (z == 1) | (z == 2)
    outer = (z == 0) | (z == 3)
    mi = lax.rem(z + 1, 2)
    mine_y, their_y = pl.multiple_of(y * Q, 16), pl.multiple_of((1 - y) * Q, 16)
    mine_m, their_m = pl.multiple_of(2 * Q + mi * Q, 16), pl.multiple_of(2 * Q + (1 - mi) * Q, 16)
    mine_y, their_y, mine_m, their_m = (pl.ds(start, Q) for start in (mine_y, their_y, mine_m, their_m))
    low = pl.ds(2 * Q, 2 * Q)

    def loads():
        pairs = ((x.at[0], H), (wg.at[0], WF), (wu.at[0], WU), (wd.at[0], WFD), (dy.at[0], DY))
        return [pltpu.make_async_copy(s, d, ld.at[i]) for i, (s, d) in enumerate(pairs)]

    def weights(i):
        layer, j, s = L - 1 - i // PER, lax.rem(i, PER), lax.rem(i, 2)
        cols = pl.ds(pl.multiple_of(j * C, C), C)
        return [
            pltpu.make_async_copy(wg.at[layer, :, cols], WGU.at[s, :, pl.ds(0, C)], ws.at[s, 0]),
            pltpu.make_async_copy(wu.at[layer, :, cols], WGU.at[s, :, pl.ds(C, C)], ws.at[s, 1]),
            pltpu.make_async_copy(wd.at[layer, cols, :], WD.at[s], ws.at[s, 2]),
        ]

    for copy in loads() + weights(0):
        copy.start()

    barrier = pltpu.get_barrier_semaphore()
    for device in (partner, across, end):
        pl.semaphore_signal(barrier, inc=1, device_id=device, device_id_type=MESH)

    @pl.when(inner)
    def _():
        pl.semaphore_signal(barrier, inc=1, device_id=mid, device_id_type=MESH)

    DA[...] = jnp.zeros_like(DA)
    for copy in loads():
        copy.wait()

    def forward(b, _):
        rows = pl.ds(pl.multiple_of(b * 512, 512), 512)
        x = H[rows]
        a = normed(x)
        A[0, rows] = a
        AT[0, :, rows] = a.T
        DYT[:, rows] = DY[rows].T
        for k in range(4):
            cols = pl.ds(k * 512, 512)
            gate, up = dot(a, WF[:, cols]), dot(a, WU[:, cols])
            ACTF[:, cols] = (gate * sigmoid(gate) * up).astype(BF16)
        h = add(x, dot(ACTF[...], WFD[...]).astype(BF16))
        H[rows] = h
        a = normed(h)
        A[1, rows] = a
        AT[1, :, rows] = a.T
        return _

    lax.fori_loop(0, T // 512, forward, None)
    pl.semaphore_wait(barrier, 3 + inner.astype(jnp.int32))

    def copies(q):
        def remote(n, src, dst, device):
            return pltpu.make_async_remote_copy(
                src_ref=src, dst_ref=dst, send_sem=sent.at[n, q], recv_sem=got.at[n, q], device_id=device, device_id_type=MESH
            )

        own = G.at[q, core]
        made = dict(
            d1=lambda: remote(0, G.at[q, 1 - core], DD.at[q], partner),
            y1=lambda: remote(1, ST1.at[q], YR.at[q], across),
            z2=lambda: remote(2, ST2.at[q], ZR2.at[q], end),
            z1=lambda: remote(3, ST3.at[q], ZR1.at[q], end),
            m2=lambda: remote(4, ST2.at[q, pl.ds(0, Q)], MR.at[q], mid),
            x1=lambda: remote(5, ST3.at[q], XR.at[q], mid),
            y2=lambda: remote(6, ST2.at[q, pl.ds(Q, Q)], YX.at[q], across),
            f1=lambda: remote(7, own.at[mine_y], own.at[mine_y], end),
            f2=lambda: remote(8, own.at[mine_y], own.at[mine_y], across),
            g1=lambda: remote(9, own.at[mine_m], own.at[mine_m], mid),
            g2=lambda: remote(10, own.at[mine_m], own.at[mine_m], end),
            g3=lambda: remote(11, own.at[their_m], own.at[their_m], end),
            d2=lambda: remote(12, own, own, partner),
        )
        return lambda name: made[name]()

    def out_copies(c, odd):
        layer, j, q, s = L - 1 - c // (2 * PER), lax.rem(c // 2, PER), lax.rem(c, NS), lax.rem(c // 2, 2)
        made = []
        for half in range(2):
            cols = pl.ds(pl.multiple_of(j * C + half * 128, 128), 128)
            if odd:
                made.append(pltpu.make_async_copy(G.at[q, half, pl.ds(0, D // 2)], out_u.at[layer, pl.ds(D // 2, D // 2), cols], outs.at[1, half]))
            else:
                made.append(pltpu.make_async_copy(G.at[q, half, pl.ds(0, D)], out_g.at[layer, :, cols], outs.at[0, half]))
                made.append(pltpu.make_async_copy(G.at[q, half, pl.ds(D, D // 2)], out_u.at[layer, pl.ds(0, D // 2), cols], outs.at[0, 2 + half]))
        if odd:
            rows = pl.ds(pl.multiple_of(j * C, C), C)
            made.append(pltpu.make_async_copy(OT.at[s], out_d.at[layer, rows, :], outs.at[1, 4]))
        return made

    def stage_d1(q, c):
        c("d1").start()

    def stage_first(q, c):
        c("d1").wait()
        ST1[q] = add(G[q, core, their_y], DD[q, their_y])
        c("y1").start()

        @pl.when(outer)
        def _():
            ST2[q] = add(G[q, core, low], DD[q, low])
            c("z2").start()

    def stage_z1(q, c):
        @pl.when(outer)
        def _():
            c("y1").wait_recv()
            ST3[q] = add(G[q, core, mine_y], DD[q, mine_y], YR[q])
            c("z1").start()

    def stage_m2(q, c):
        @pl.when(inner)
        def _():
            c("z2").wait_recv()
            ST2[q, pl.ds(0, Q)] = add(G[q, core, their_m], DD[q, their_m], ZR2[q, pl.ds(pl.multiple_of((1 - mi) * Q, 16), Q)])
            c("m2").start()

    def stage_x1(q, c):
        @pl.when(inner)
        def _():
            c("y1").wait_recv()
            c("z1").wait_recv()
            ST3[q] = add(G[q, core, mine_y], DD[q, mine_y], YR[q], ZR1[q])
            c("x1").start()

    def stage_y2(q, c):
        @pl.when(inner)
        def _():
            c("m2").wait_recv()
            ST2[q, pl.ds(Q, Q)] = add(G[q, core, mine_m], DD[q, mine_m], ZR2[q, pl.ds(pl.multiple_of(mi * Q, 16), Q)], MR[q])
            c("y2").start()

    def stage_f(q, c):
        @pl.when(inner)
        def _():
            c("x1").wait()
            G[q, core, mine_y] = add(ST3[q], XR[q])
            c("f1").start()
            c("f2").start()

    def stage_g(q, c):
        @pl.when(inner)
        def _():
            c("y2").wait()
            G[q, core, mine_m] = add(ST2[q, pl.ds(Q, Q)], YX[q])
            c("g1").start()
            c("g2").start()

    def stage_f2(q, c):
        @pl.when(outer)
        def _():
            c("f1").wait_recv()
            c("f2").start()

    def stage_g3(q, c):
        @pl.when(inner)
        def _():
            c("g1").wait_recv()
            c("g3").start()

    def stage_d2(q, c):
        c("f2").wait_recv()

        @pl.when(outer)
        def _():
            c("g2").wait_recv()
            c("g3").wait_recv()

        c("d2").start()

    def stage_end(q, c):
        c("d2").wait()
        for name in ("y1", "f2"):
            c(name).wait_send()

        @pl.when(outer)
        def _():
            for name in ("z2", "z1"):
                c(name).wait_send()

        @pl.when(inner)
        def _():
            for name in ("m2", "f1", "g1", "g2", "g3"):
                c(name).wait_send()

    STAGES = {
        0: stage_d1, 1: stage_first, 3: stage_z1, 4: stage_m2, 5: stage_x1, 6: stage_y2,
        7: stage_f, 8: stage_g, 9: stage_f2, 10: stage_g3, 12: stage_d2,
    }
    END = 13

    def finish(c, odd):
        q, s = lax.rem(c, NS), lax.rem(c // 2, 2)

        @pl.when(c >= 1)
        def _():
            for copy in out_copies(c - 1, not odd):
                copy.wait()

        stage_end(q, copies(q))
        if odd:
            for half in range(2):
                OT[s, pl.ds(half * 128, 128), :] = G[q, half, pl.ds(D // 2, D)].T
        for copy in out_copies(c, odd):
            copy.start()

    def tick(u, k):
        for when, stage in sorted(STAGES.items(), reverse=True):
            if when % 2 != k:
                continue
            c = u - 2 - when // 2

            @pl.when((c >= 0) & (c < PIECES))
            def _(c=c, stage=stage):
                q = lax.rem(c, NS)
                stage(q, copies(q))

        if END % 2 == k:
            c = u - 2 - END // 2
            for odd in (False, True):

                @pl.when((c >= 0) & (c < PIECES) & (lax.rem(c + 2, 2) == int(odd)))
                def _(odd=odd):
                    finish(c, odd)

    def tokens(s, layer, first):
        for b in range(2):
            rows = pl.ds(first + b * 512, 512)
            gu = dot(A[layer, rows], WGU[s])
            gate, up = gu[:, :C], gu[:, C:]
            dact = dot_nt(DY[rows], WD[s]).astype(BF16).astype(F32)
            sig = sigmoid(gate)
            silu = gate * sig
            ACT[rows] = (silu * up).astype(BF16)
            DGU[rows, pl.ds(0, C)] = (dact * up * (sig + silu * (1.0 - sig))).astype(BF16)
            DGU[rows, pl.ds(C, C)] = (dact * silu).astype(BF16)

    def switch():
        def block(b, _):
            rows = pl.ds(pl.multiple_of(b * 256, 256), 256)
            h = H[rows].astype(F32)
            da = DA[rows].astype(BF16).astype(F32)
            scale = lax.rsqrt(jnp.mean(h * h, -1, keepdims=True) + 1e-6)
            along = jnp.sum(da * h, -1, keepdims=True) * (1.0 / D)
            dh = (scale * (da - h * (scale * scale * along))).astype(BF16)
            new = add(DY[rows], dh)
            DY[rows] = new
            DYT[:, rows] = new.T
            return _

        lax.fori_loop(0, T // 256, block, None)

    def step(u, _):
        i = u // 2
        busy = i < N
        even, odd = busy & (lax.rem(u, 2) == 0), busy & (lax.rem(u, 2) == 1)
        s, layer = lax.rem(i, 2), jnp.maximum(L - 1 - i // PER, 0)
        first, second = lax.rem(2 * i, NS), lax.rem(2 * i + 1, NS)

        tick(u, 0)

        @pl.when(u == 2 * PER)
        def _():
            switch()

        @pl.when(even)
        def _():
            for copy in weights(i):
                copy.wait()

            @pl.when(i + 1 < N)
            def _():
                for copy in weights(i + 1):
                    copy.start()

            tokens(s, layer, 0)

        @pl.when(odd)
        def _():
            g = dot(AT[layer], DGU[...]).astype(BF16)
            for half in range(2):
                cols = slice(half * 128, half * 128 + 128)
                G[first, half, pl.ds(0, D)] = g[:, cols]
                cols = slice(C + half * 128, C + half * 128 + 128)
                G[first, half, pl.ds(D, D // 2)] = g[: D // 2, cols]
                G[second, half, pl.ds(0, D // 2)] = g[D // 2 :, cols]

        tick(u, 1)

        @pl.when(even)
        def _():
            tokens(s, layer, T // 2)

        @pl.when(odd)
        def _():
            g = dot(DYT[...], ACT[...]).astype(BF16)
            for half in range(2):
                G[second, half, pl.ds(D // 2, D)] = g[:, half * 128 : half * 128 + 128]

        @pl.when(odd & (i < PER))
        def _():
            for b in range(2):
                rows = pl.ds(b * 1024, 1024)
                DA[rows] += dot_nt(DGU[rows], WGU[s])

        return _

    lax.fori_loop(0, PIECES + 2 + END // 2 + 1, step, None)
    for copy in out_copies(PIECES - 1, True):
        copy.wait()


def gradients_of(x, dy, wg, wu, wd):
    vm, dma = pltpu.VMEM, pltpu.SemaphoreType.DMA
    return pl.pallas_call(
        step_kernel,
        out_shape=[jax.ShapeDtypeStruct(w.shape, BF16) for w in (wg, wu, wd)],
        in_specs=[pl.BlockSpec(memory_space=pl.ANY)] * 5,
        out_specs=[pl.BlockSpec(memory_space=pl.ANY)] * 3,
        scratch_shapes=[
            vm((L, T, D), BF16), vm((L, D, T), BF16), vm((T, D), BF16), vm((D, T), BF16), vm((T, D), BF16), vm((T, D), F32),
            vm((T, C), BF16), vm((T, 2 * C), BF16), vm((512, FF), BF16),
            vm((D, FF), BF16), vm((D, FF), BF16), vm((FF, D), BF16),
            vm((2, D, 2 * C), BF16), vm((2, C, D), BF16), vm((2, C, D), BF16),
            vm((NS, 2, R, 128), BF16), vm((NS, R, 128), BF16), vm((NS, Q, 128), BF16), vm((NS, Q, 128), BF16), vm((NS, Q, 128), BF16),
            vm((NS, 2 * Q, 128), BF16), vm((NS, Q, 128), BF16), vm((NS, Q, 128), BF16),
            vm((NS, Q, 128), BF16), vm((NS, 2 * Q, 128), BF16), vm((NS, Q, 128), BF16),
            dma((5,)), dma((2, 3)), dma((2, 5)), dma((13, NS)), dma((13, NS)),
        ],
        compiler_params=pltpu.CompilerParams(collective_id=0, has_side_effects=True, vmem_limit_bytes=67043328),
    )(x, dy, wg, wu, wd)


def adamw(w, m, v, g):
    m = 0.9 * m + 0.1 * g
    v = 0.95 * v + 0.05 * g * g
    step = m * lax.rsqrt(v + 1e-8) + 0.1 * w
    return (w - 0.02 * step).astype(BF16), m, v


def solution(mesh):
    def step(x, dy, *arrays):
        weights, m, v = (arrays[i : i + 3] for i in (0, 3, 6))
        gradients = gradients_of(x, dy, *weights)
        new = [adamw(w.astype(F32), m, v, g.astype(F32)) for w, m, v, g in zip(weights, m, v, gradients, strict=True)]
        return tuple(one[which] for which in range(3) for one in new)

    return jax.shard_map(
        step,
        mesh=mesh,
        in_specs=(P(("rep", "dp"), None, None),) * 2 + (P(None, None, None),) * 9,
        out_specs=(P("rep", None, None),) * 9,
        check_vma=False,
    )
```

time: 342 us -> 266 us (0.78)
  matrix products: 31.9 us -> 0 us
  local copies, waits for them, and re-layouts: 20.5 us -> 0 us
  other arithmetic: 74.5 us -> 61.9 us
  Pallas kernels: 214 us -> 203 us
    dot_general x2 -> x0, matrix products: 31.9 us -> none  [dot(): return jnp.dot(a, b, preferred_element_type=F32)]
    pallas_call x1, Pallas kernels: 214 us -> 203 us  [gradients_of(): pl.pallas_call(step_kernel, out_shape=[jax.ShapeDtypeStruct(w.shape, BF16...]
    convert_element_type x2 -> x0, local copies, waits for them, and re-layouts: 8.75 us -> none  [normed(): return (wide * scale).astype(BF16)]
    unnamed x2 -> x0, local copies, waits for them, and re-layouts: 7.37 us -> none
    transpose x2 -> x0, other arithmetic: 6.1 us -> none  [step(): gradients = backward(a1, a1.T, dy, dy.T, h1, a0, a0.T, wg, wu, wd)]
    convert_element_type x2 -> x0, other arithmetic: 6.09 us -> none  [normed(): return (wide * scale).astype(BF16)]
    add x1 -> x0, local copies, waits for them, and re-layouts: 4.37 us -> none  [step(): h1 = x + dot(act, wd[0]).astype(BF16)]
where the time goes in v2:
time: 266 us
  Pallas kernels  203 us (76%)
  other arithmetic  61.9 us (23%)
    pallas_call x1, Pallas kernels, gradients_of(): pl.pallas_call(step_kernel, out_shape=[jax.ShapeDtypeStruct(w.shape, BF16...  203 us
    convert_element_type x2, other arithmetic, adamw(): return ((w - 0.02 * step).astype(BF16), m, v)  61.9 us

profile of v2, /device:TPU:0, one launch (start us, length us, event | category | flops | bytes accessed | tf_op | source)
XLA Modules:
  0.0 265.8 jit_solution(256241920849962954)
XLA Ops:
  0.6 203.3 %shard_map.178 = (bf16[2,640,2048]{2,1,0:T(8,128)(2,1)}, bf16[2,640,2048]{2,1,0:T(8,128)(2,1)}, bf16[2,2048,640]{2,1,0:T(8,128)(2,1)}) custom-call(bf16[1,2048,640]{2,1,0:T(8,128)(2,1)} %x.1, bf16[1,2048,640]{2,1,0:T(8,128)(2,1)} %dy.1, bf16[2,640,2048]{2,1,0:T(8,128)(2,1)} %wg.1, bf16[2,640,2048]{2,1,0:T(8,128)(2,1)} %wu.1, bf16[2,2048,640]{2,1,0:T(8,128)(2,1)} %wd.1), custom_call_target="tpu_custom_call" | custom-call | tf_op jit(solution)/shard_map/pallas_call | solution.py:378
  203.9 40.1 %fusion.2 = (bf16[2,640,2048]{2,1,0:T(8,128)(2,1)}, f32[2,640,2048]{2,1,0:T(8,128)}, f32[2,640,2048]{2,1,0:T(8,128)}, bf16[2,640,2048]{2,1,0:T(8,128)(2,1)}, f32...) fusion(bf16[2,640,2048]{2,1,0:T(8,128)(2,1)} %wg.1, bf16[2,640,2048]{2,1,0:T(8,128)(2,1)} %get-tuple-element.12, ...), kind=kLoop, calls=%fused_computation.14 | loop fusion | flops 83886080 | bytes 115343360 | tf_op jit(solution)/shard_map/convert_element_type | solution.py:401
  244.0 21.8 %fusion.10 = (bf16[2,2048,640]{2,1,0:T(8,128)(2,1)}, f32[2,2048,640]{2,1,0:T(8,128)}, f32[2,2048,640]{2,1,0:T(8,128)}) fusion(bf16[2,2048,640]{2,1,0:T(8,128)(2,1)} %wd.1, bf16[2,2048,640]{2,1,0:T(8,128)(2,1)} %get-tuple-element.14, f32[2,2048,640]{2,1,0:T(8,128)} %param.21, f32[2,2048,640]{2,1,0:T(8,128)} %param.18), kind=kLoop, calls=%fused_computation.22 | loop fusion | flops 41943040 | bytes 57671680 | tf_op jit(solution)/shard_map/convert_element_type | solution.py:401

commit v3 on v2

--- a/solution.py
+++ b/solution.py
@@ -12,7 +12,7 @@
 PER = FF // C
 N = L * PER
 PIECES = 2 * N
-NS = 10
+NS = 12
 R = 3 * D // 2
 Q = R // 4
 MESH = pl.DeviceIdType.MESH
@@ -64,7 +64,12 @@
     low = pl.ds(2 * Q, 2 * Q)
 
     def loads():
-        pairs = ((x.at[0], H), (wg.at[0], WF), (wu.at[0], WU), (wd.at[0], WFD), (dy.at[0], DY))
+        start, rest = pl.ds(0, 512), pl.ds(512, T - 512)
+        pairs = [(x.at[0, start], H.at[start])]
+        for k in range(4):
+            cols = pl.ds(k * 512, 512)
+            pairs += [(wg.at[0, :, cols], WF.at[:, cols]), (wu.at[0, :, cols], WU.at[:, cols])]
+        pairs += [(wd.at[0], WFD), (dy.at[0], DY), (x.at[0, rest], H.at[rest])]
         return [pltpu.make_async_copy(s, d, ld.at[i]) for i, (s, d) in enumerate(pairs)]
 
     def weights(i):
@@ -76,7 +81,8 @@
             pltpu.make_async_copy(wd.at[layer, cols, :], WD.at[s], ws.at[s, 2]),
         ]
 
-    for copy in loads() + weights(0):
+    arriving = loads()
+    for copy in arriving + weights(0):
         copy.start()
 
     barrier = pltpu.get_barrier_semaphore()
@@ -87,29 +93,37 @@
     def _():
         pl.semaphore_signal(barrier, inc=1, device_id=mid, device_id_type=MESH)
 
-    DA[...] = jnp.zeros_like(DA)
-    for copy in loads():
-        copy.wait()
-
-    def forward(b, _):
-        rows = pl.ds(pl.multiple_of(b * 512, 512), 512)
+    def forward(rows, wait):
+        wait(0, 1)
         x = H[rows]
         a = normed(x)
         A[0, rows] = a
         AT[0, :, rows] = a.T
-        DYT[:, rows] = DY[rows].T
         for k in range(4):
+            wait(2 * k + 1, 2 * k + 3)
             cols = pl.ds(k * 512, 512)
             gate, up = dot(a, WF[:, cols]), dot(a, WU[:, cols])
             ACTF[:, cols] = (gate * sigmoid(gate) * up).astype(BF16)
+        wait(9, 11)
+        DYT[:, rows] = DY[rows].T
+        DA[rows] = jnp.zeros((512, D), F32)
         h = add(x, dot(ACTF[...], WFD[...]).astype(BF16))
         H[rows] = h
         a = normed(h)
         A[1, rows] = a
         AT[1, :, rows] = a.T
+
+    def now(first, last):
+        for copy in arriving[first:last]:
+            copy.wait()
+
+    def later(b, _):
+        forward(pl.ds(pl.multiple_of(b * 512, 512), 512), lambda first, last: None)
         return _
 
-    lax.fori_loop(0, T // 512, forward, None)
+    forward(pl.ds(0, 512), now)
+    now(11, 12)
+    lax.fori_loop(1, T // 512, later, None)
     pl.semaphore_wait(barrier, 3 + inner.astype(jnp.int32))
 
     def copies(q):
@@ -247,10 +261,10 @@
                 c(name).wait_send()
 
     STAGES = {
-        0: stage_d1, 1: stage_first, 3: stage_z1, 4: stage_m2, 5: stage_x1, 6: stage_y2,
-        7: stage_f, 8: stage_g, 9: stage_f2, 10: stage_g3, 12: stage_d2,
+        0: (stage_d1,), 1: (stage_first,), 4: (stage_z1,), 5: (stage_m2,), 8: (stage_x1, stage_y2),
+        11: (stage_f, stage_g), 14: (stage_f2, stage_g3), 17: (stage_d2,),
     }
-    END = 13
+    END = 18
 
     def finish(c, odd):
         q, s = lax.rem(c, NS), lax.rem(c // 2, 2)
@@ -268,15 +282,16 @@
             copy.start()
 
     def tick(u, k):
-        for when, stage in sorted(STAGES.items(), reverse=True):
+        for when, stages in sorted(STAGES.items(), reverse=True):
             if when % 2 != k:
                 continue
             c = u - 2 - when // 2
 
             @pl.when((c >= 0) & (c < PIECES))
-            def _(c=c, stage=stage):
+            def _(c=c, stages=stages):
                 q = lax.rem(c, NS)
-                stage(q, copies(q))
+                for stage in stages:
+                    stage(q, copies(q))
 
         if END % 2 == k:
             c = u - 2 - END // 2
@@ -354,8 +369,7 @@
         def _():
             tokens(s, layer, T // 2)
 
-        @pl.when(odd)
-        def _():
+        def down():
             g = dot(DYT[...], ACT[...]).astype(BF16)
             for half in range(2):
                 G[second, half, pl.ds(D // 2, D)] = g[:, half * 128 : half * 128 + 128]
@@ -365,6 +379,11 @@
             for b in range(2):
                 rows = pl.ds(b * 1024, 1024)
                 DA[rows] += dot_nt(DGU[rows], WGU[s])
+            down()
+
+        @pl.when(odd & (i >= PER))
+        def _():
+            down()
 
         return _
 
@@ -388,7 +407,7 @@
             vm((NS, 2, R, 128), BF16), vm((NS, R, 128), BF16), vm((NS, Q, 128), BF16), vm((NS, Q, 128), BF16), vm((NS, Q, 128), BF16),
             vm((NS, 2 * Q, 128), BF16), vm((NS, Q, 128), BF16), vm((NS, Q, 128), BF16),
             vm((NS, Q, 128), BF16), vm((NS, 2 * Q, 128), BF16), vm((NS, Q, 128), BF16),
-            dma((5,)), dma((2, 3)), dma((2, 5)), dma((13, NS)), dma((13, NS)),
+            dma((12,)), dma((2, 3)), dma((2, 5)), dma((13, NS)), dma((13, NS)),
         ],
         compiler_params=pltpu.CompilerParams(collective_id=0, has_side_effects=True, vmem_limit_bytes=67043328),
     )(x, dy, wg, wu, wd)
@@ -401,12 +420,30 @@
     return (w - 0.02 * step).astype(BF16), m, v
 
 
+def update_kernel(*refs):
+    w, m, v, g, new_w, new_m, new_v = (refs[i : i + 3] for i in range(0, 21, 3))
+    for k in range(3):
+        new_w[k][...], new_m[k][...], new_v[k][...] = adamw(w[k][...].astype(F32), m[k][...], v[k][...], g[k][...].astype(F32))
+
+
+def update(w, m, v, g):
+    parts = 8
+    blocks = [pl.BlockSpec((1, a.shape[1] // parts, a.shape[2]), lambda i: (i // parts, lax.rem(i, parts), 0)) for a in w]
+    return pl.pallas_call(
+        update_kernel,
+        grid=(L * parts,),
+        out_shape=[jax.ShapeDtypeStruct(a.shape, kind) for kind in (BF16, F32, F32) for a in w],
+        in_specs=blocks * 4,
+        out_specs=blocks * 3,
+        compiler_params=pltpu.CompilerParams(vmem_limit_bytes=67043328),
+    )(*w, *m, *v, *g)
+
+
 def solution(mesh):
     def step(x, dy, *arrays):
         weights, m, v = (arrays[i : i + 3] for i in (0, 3, 6))
         gradients = gradients_of(x, dy, *weights)
-        new = [adamw(w.astype(F32), m, v, g.astype(F32)) for w, m, v, g in zip(weights, m, v, gradients, strict=True)]
-        return tuple(one[which] for which in range(3) for one in new)
+        return tuple(update(weights, m, v, gradients))
 
     return jax.shard_map(
         step,

time: 266 us -> 252 us (0.947)
  other arithmetic: 61.9 us -> 0 us
  Pallas kernels: 203 us -> 252 us
    convert_element_type x2 -> x0, other arithmetic: 61.9 us -> none  [adamw(): return ((w - 0.02 * step).astype(BF16), m, v)]
    pallas_call x0 -> x1, Pallas kernels: none -> 58.1 us  [update(): pl.pallas_call(update_kernel, grid=(L * parts,), out_shape=[jax.ShapeDtyp...]
    pallas_call x1, Pallas kernels: 203 us -> 193 us  [gradients_of(): pl.pallas_call(step_kernel, out_shape=[jax.ShapeDtypeStruct(w.shape, BF16...]
where the time goes in v3:
time: 252 us
  Pallas kernels  252 us (100%)
    pallas_call x1, Pallas kernels, gradients_of(): pl.pallas_call(step_kernel, out_shape=[jax.ShapeDtypeStruct(w.shape, BF16...  193 us
    pallas_call x1, Pallas kernels, update(): pl.pallas_call(update_kernel, grid=(L * parts,), out_shape=[jax.ShapeDtyp...  58.1 us

profile of v3, /device:TPU:0, one launch (start us, length us, event | category | flops | bytes accessed | tf_op | source)
XLA Modules:
  0.0 252.3 jit_solution(13208457409840400479)
XLA Ops:
  0.6 193.5 %shard_map.178 = (bf16[2,640,2048]{2,1,0:T(8,128)(2,1)}, bf16[2,640,2048]{2,1,0:T(8,128)(2,1)}, bf16[2,2048,640]{2,1,0:T(8,128)(2,1)}) custom-call(bf16[1,2048,640]{2,1,0:T(8,128)(2,1)} %x.1, bf16[1,2048,640]{2,1,0:T(8,128)(2,1)} %dy.1, bf16[2,640,2048]{2,1,0:T(8,128)(2,1)} %refs_0_.1, bf16[2,640,2048]{2,1,0:T(8,128)(2,1)} %refs_1_.1, ...), custom_call_target="tpu_custom_call" | custom-call | tf_op jit(solution)/shard_map/pallas_call | solution.py:397
  194.1 58.1 %shard_map.179 = (bf16[2,640,2048]{2,1,0:T(8,128)(2,1)}, bf16[2,640,2048]{2,1,0:T(8,128)(2,1)}, bf16[2,2048,640]{2,1,0:T(8,128)(2,1)}, f32[2,640,2048]{2,1,0:T(8...) custom-call(bf16[2,640,2048]{2,1,0:T(8,128)(2,1)} %refs_0_.1, ...), custom_call_target="tpu_custom_call" | custom-call | tf_op jit(solution)/shard_map/pallas_call | solution.py:432

commit v4 on v3

--- a/solution.py
+++ b/solution.py
@@ -45,10 +45,10 @@
 
 
 def step_kernel(
-    x, dy, wg, wu, wd, out_g, out_u, out_d,
-    A, AT, DY, DYT, H, DA, ACT, DGU, ACTF, WF, WU, WFD, WGU, WD, OT,
+    x, dy, wg, wu, wd, md, out_g, out_u, out_d, WF, WU, WFD, H, DA,
+    A, AT, DY, DYT, ACT, DGU, ACTF, WGU, WD, OT,
     G, DD, YR, ZR1, XR, ZR2, MR, YX, ST1, ST2, ST3,
-    ld, ws, outs, sent, got,
+    ld, ws, outs, sent, got, kept,
 ):
     rep, dp = lax.axis_index("rep"), lax.axis_index("dp")
     core, z, y = lax.rem(dp, 2), lax.rem(dp // 2, 4), dp // 8
@@ -84,6 +84,10 @@
     arriving = loads()
     for copy in arriving + weights(0):
         copy.start()
+
+    def keep(n):
+        source, target = ((wd.at[1], H), (md.at[1], DA))[n]
+        return pltpu.make_async_copy(source, target, kept.at[n])
 
     barrier = pltpu.get_barrier_semaphore()
     for device in (partner, across, end):
@@ -261,8 +265,8 @@
                 c(name).wait_send()
 
     STAGES = {
-        0: (stage_d1,), 1: (stage_first,), 4: (stage_z1,), 5: (stage_m2,), 8: (stage_x1, stage_y2),
-        11: (stage_f, stage_g), 14: (stage_f2, stage_g3), 17: (stage_d2,),
+        0: (stage_d1,), 1: (stage_first,), 3: (stage_z1,), 5: (stage_m2,), 6: (stage_x1,), 8: (stage_y2,),
+        9: (stage_f,), 11: (stage_g,), 12: (stage_f2,), 14: (stage_g3,), 17: (stage_d2,),
     }
     END = 18
 
@@ -340,6 +344,8 @@
         @pl.when(u == 2 * PER)
         def _():
             switch()
+            for n in range(2):
+                keep(n).start()
 
         @pl.when(even)
         def _():
@@ -388,29 +394,29 @@
         return _
 
     lax.fori_loop(0, PIECES + 2 + END // 2 + 1, step, None)
-    for copy in out_copies(PIECES - 1, True):
+    for copy in out_copies(PIECES - 1, True) + [keep(n) for n in range(2)]:
         copy.wait()
 
 
-def gradients_of(x, dy, wg, wu, wd):
+def gradients_of(x, dy, wg, wu, wd, md):
     vm, dma = pltpu.VMEM, pltpu.SemaphoreType.DMA
     return pl.pallas_call(
         step_kernel,
-        out_shape=[jax.ShapeDtypeStruct(w.shape, BF16) for w in (wg, wu, wd)],
-        in_specs=[pl.BlockSpec(memory_space=pl.ANY)] * 5,
-        out_specs=[pl.BlockSpec(memory_space=pl.ANY)] * 3,
+        out_shape=[jax.ShapeDtypeStruct(w.shape, BF16) for w in (wg, wu, wd)]
+        + [vm((D, FF), BF16), vm((D, FF), BF16), vm((FF, D), BF16), vm((T, D), BF16), vm((T, D), F32)],
+        in_specs=[pl.BlockSpec(memory_space=pl.ANY)] * 6,
+        out_specs=[pl.BlockSpec(memory_space=pl.ANY)] * 3 + [pl.BlockSpec(memory_space=vm)] * 5,
         scratch_shapes=[
-            vm((L, T, D), BF16), vm((L, D, T), BF16), vm((T, D), BF16), vm((D, T), BF16), vm((T, D), BF16), vm((T, D), F32),
+            vm((L, T, D), BF16), vm((L, D, T), BF16), vm((T, D), BF16), vm((D, T), BF16),
             vm((T, C), BF16), vm((T, 2 * C), BF16), vm((512, FF), BF16),
-            vm((D, FF), BF16), vm((D, FF), BF16), vm((FF, D), BF16),
             vm((2, D, 2 * C), BF16), vm((2, C, D), BF16), vm((2, C, D), BF16),
             vm((NS, 2, R, 128), BF16), vm((NS, R, 128), BF16), vm((NS, Q, 128), BF16), vm((NS, Q, 128), BF16), vm((NS, Q, 128), BF16),
             vm((NS, 2 * Q, 128), BF16), vm((NS, Q, 128), BF16), vm((NS, Q, 128), BF16),
             vm((NS, Q, 128), BF16), vm((NS, 2 * Q, 128), BF16), vm((NS, Q, 128), BF16),
-            dma((12,)), dma((2, 3)), dma((2, 5)), dma((13, NS)), dma((13, NS)),
+            dma((12,)), dma((2, 3)), dma((2, 5)), dma((13, NS)), dma((13, NS)), dma((2,)),
         ],
-        compiler_params=pltpu.CompilerParams(collective_id=0, has_side_effects=True, vmem_limit_bytes=67043328),
-    )(x, dy, wg, wu, wd)
+        compiler_params=pltpu.CompilerParams(collective_id=0, has_side_effects=True, vmem_limit_bytes=51 * 10**6),
+    )(x, dy, wg, wu, wd, md)
 
 
 def adamw(w, m, v, g):
@@ -420,30 +426,48 @@
     return (w - 0.02 * step).astype(BF16), m, v
 
 
+PARTS = 8
+
+
 def update_kernel(*refs):
-    w, m, v, g, new_w, new_m, new_v = (refs[i : i + 3] for i in range(0, 21, 3))
-    for k in range(3):
-        new_w[k][...], new_m[k][...], new_v[k][...] = adamw(w[k][...].astype(F32), m[k][...], v[k][...], g[k][...].astype(F32))
-
-
-def update(w, m, v, g):
-    parts = 8
-    blocks = [pl.BlockSpec((1, a.shape[1] // parts, a.shape[2]), lambda i: (i // parts, lax.rem(i, parts), 0)) for a in w]
+    w0, (w1_down, m1_down), w1 = refs[0:3], refs[3:5], refs[5:7]
+    m, v, g, new_w, new_m, new_v = (refs[i : i + 3] for i in range(7, 25, 3))
+    layer, part = pl.program_id(0) // PARTS, lax.rem(pl.program_id(0), PARTS)
+    wide = pl.ds(pl.multiple_of(part * (D // PARTS), D // PARTS), D // PARTS)
+    tall = pl.ds(pl.multiple_of(part * (FF // PARTS), FF // PARTS), FF // PARTS)
+
+    def step(w, old_m):
+        for k in range(3):
+            new_w[k][0], new_m[k][0], new_v[k][0] = adamw(w[k].astype(F32), old_m[k], v[k][0], g[k][0].astype(F32))
+
+    @pl.when(layer == 0)
+    def _():
+        step((w0[0][wide], w0[1][wide], w0[2][tall]), (m[0][0], m[1][0], m[2][0]))
+
+    @pl.when(layer == 1)
+    def _():
+        step((w1[0][0], w1[1][0], w1_down[tall]), (m[0][0], m[1][0], m1_down[tall]))
+
+
+def update(kept, w, m, v, g):
+    blocks = [pl.BlockSpec((1, a.shape[1] // PARTS, a.shape[2]), lambda i: (i // PARTS, lax.rem(i, PARTS), 0)) for a in m]
+    first = pl.BlockSpec((1, FF // PARTS, D), lambda i: (0, jnp.minimum(i, PARTS - 1), 0))
+    second = pl.BlockSpec((1, D // PARTS, FF), lambda i: (1, jnp.maximum(i - PARTS, 0), 0))
     return pl.pallas_call(
         update_kernel,
-        grid=(L * parts,),
-        out_shape=[jax.ShapeDtypeStruct(a.shape, kind) for kind in (BF16, F32, F32) for a in w],
-        in_specs=blocks * 4,
+        grid=(L * PARTS,),
+        out_shape=[jax.ShapeDtypeStruct(a.shape, kind) for kind in (BF16, F32, F32) for a in m],
+        in_specs=[pl.BlockSpec(memory_space=pltpu.VMEM)] * 5 + [second] * 2 + blocks[:2] + [first] + blocks * 2,
         out_specs=blocks * 3,
-        compiler_params=pltpu.CompilerParams(vmem_limit_bytes=67043328),
-    )(*w, *m, *v, *g)
+        compiler_params=pltpu.CompilerParams(vmem_limit_bytes=38 * 10**6),
+    )(*kept, *w[:2], *m, *v, *g)
 
 
 def solution(mesh):
     def step(x, dy, *arrays):
         weights, m, v = (arrays[i : i + 3] for i in (0, 3, 6))
-        gradients = gradients_of(x, dy, *weights)
-        return tuple(update(weights, m, v, gradients))
+        gathered = gradients_of(x, dy, *weights, m[2])
+        return tuple(update(gathered[3:], weights, m, v, gathered[:3]))
 
     return jax.shard_map(
         step,

time: 252 us -> 249 us (0.988)
  Pallas kernels: 252 us -> 248 us
    pallas_call x1, Pallas kernels: 58.1 us -> 55.2 us  [update(): pl.pallas_call(update_kernel, grid=(L * PARTS,), out_shape=[jax.ShapeDtyp...]
where the time goes in v4:
time: 249 us
  Pallas kernels  248 us (100%)
    pallas_call x1, Pallas kernels, gradients_of(): pl.pallas_call(step_kernel, out_shape=[jax.ShapeDtypeStruct(w.shape, BF16...  193 us
    pallas_call x1, Pallas kernels, update(): pl.pallas_call(update_kernel, grid=(L * PARTS,), out_shape=[jax.ShapeDtyp...  55.2 us

profile of v4, /device:TPU:0, one launch (start us, length us, event | category | flops | bytes accessed | tf_op | source)
XLA Modules:
  0.0 248.6 jit_solution(11365740140218132071)
XLA Ops:
  0.6 192.6 %shard_map.178 = (bf16[2,640,2048]{2,1,0:T(8,128)(2,1)}, bf16[2,640,2048]{2,1,0:T(8,128)(2,1)}, bf16[2,2048,640]{2,1,0:T(8,128)(2,1)}, bf16[640,2048]{1,0:T(8,12...) custom-call(bf16[1,2048,640]{2,1,0:T(8,128)(2,1)} %x.1, ...), custom_call_target="tpu_custom_call" | custom-call | tf_op jit(solution)/shard_map/pallas_call | solution.py:403
  193.2 55.2 %shard_map.179 = (bf16[2,640,2048]{2,1,0:T(8,128)(2,1)}, bf16[2,640,2048]{2,1,0:T(8,128)(2,1)}, bf16[2,2048,640]{2,1,0:T(8,128)(2,1)}, f32[2,640,2048]{2,1,0:T(8...) custom-call(bf16[640,2048]{1,0:T(8,128)(2,1)S(1)} %get-tuple-element, ...), custom_call_target="tpu_custom_call" | custom-call | tf_op jit(solution)/shard_map/pallas_call | solution.py:456

commit v5 on v4

--- a/solution.py
+++ b/solution.py
@@ -287,9 +287,9 @@
 
     def tick(u, k):
         for when, stages in sorted(STAGES.items(), reverse=True):
-            if when % 2 != k:
+            if when % 2 == k:
                 continue
-            c = u - 2 - when // 2
+            c = u - (when + 3 - k) // 2
 
             @pl.when((c >= 0) & (c < PIECES))
             def _(c=c, stages=stages):
@@ -297,8 +297,8 @@
                 for stage in stages:
                     stage(q, copies(q))
 
-        if END % 2 == k:
-            c = u - 2 - END // 2
+        if END % 2 != k:
+            c = u - (END + 3 - k) // 2
             for odd in (False, True):
 
                 @pl.when((c >= 0) & (c < PIECES) & (lax.rem(c + 2, 2) == int(odd)))
@@ -393,7 +393,7 @@
 
         return _
 
-    lax.fori_loop(0, PIECES + 2 + END // 2 + 1, step, None)
+    lax.fori_loop(0, PIECES + (END + 2) // 2, step, None)
     for copy in out_copies(PIECES - 1, True) + [keep(n) for n in range(2)]:
         copy.wait()
 

time: 249 us -> 247 us (level)
  no operation moved by 1% of the time
where the time goes in v5:
time: 247 us
  Pallas kernels  246 us (100%)
    pallas_call x1, Pallas kernels, gradients_of(): pl.pallas_call(step_kernel, out_shape=[jax.ShapeDtypeStruct(w.shape, BF16...  191 us
    pallas_call x1, Pallas kernels, update(): pl.pallas_call(update_kernel, grid=(L * PARTS,), out_shape=[jax.ShapeDtyp...  55.2 us

profile of v5, /device:TPU:0, one launch (start us, length us, event | category | flops | bytes accessed | tf_op | source)
XLA Modules:
  0.0 247.2 jit_solution(13545649513562902872)
XLA Ops:
  0.6 191.2 %shard_map.178 = (bf16[2,640,2048]{2,1,0:T(8,128)(2,1)}, bf16[2,640,2048]{2,1,0:T(8,128)(2,1)}, bf16[2,2048,640]{2,1,0:T(8,128)(2,1)}, bf16[640,2048]{1,0:T(8,12...) custom-call(bf16[1,2048,640]{2,1,0:T(8,128)(2,1)} %x.1, ...), custom_call_target="tpu_custom_call" | custom-call | tf_op jit(solution)/shard_map/pallas_call | solution.py:403
  191.8 55.2 %shard_map.179 = (bf16[2,640,2048]{2,1,0:T(8,128)(2,1)}, bf16[2,640,2048]{2,1,0:T(8,128)(2,1)}, bf16[2,2048,640]{2,1,0:T(8,128)(2,1)}, f32[2,640,2048]{2,1,0:T(8...) custom-call(bf16[640,2048]{1,0:T(8,128)(2,1)S(1)} %get-tuple-element, ...), custom_call_target="tpu_custom_call" | custom-call | tf_op jit(solution)/shard_map/pallas_call | solution.py:456
